TPU v7x, 32 devices: a whole 2x2x4 slice. The times are simulated.
32 devices in a mesh: slab: 8 (over y, x, core), det: 4 (over z).
Axes of the slice: x: 2, y: 2, z: 4, core: 2. Of those that a mesh axis runs over, the one named last changes fastest.
Arguments:
- traces: float32 [32, 128, 4096], P(('slab', 'det')), may hold values from -6 to 6
- tables: bfloat16 [32, 256, 2048], P('slab', None, 'det'), may hold values from -0.0625 to 0.0625
- slab_range: int32 [32, 2], P(('slab', 'det')), may hold values from 0 to 7, as said below
- table_slot: int32 [32, 7], P(('slab', 'det')), may hold values from 0 to 3
- sample_start: int32 [32, 7], P(('slab', 'det')), may hold values from 0 to 3840
Outputs:
- image: float32 [128, 16384], P(None, ('slab', 'det'))
Inputs may be any that keep to these rules, and one draw needn't show every extreme that they name: For detector d with home slab g = d // 4: max(0, g - 3) <= slab_range[d, 0] <= g <= slab_range[d, 1] <= min(7, g + 3); some detectors reach the full 3 on both sides where the grid allows.
All inputs are finite; a program needn't handle non-finite values.
Results may differ from a plain program's by a relative error of at most 0.007.
Values may be sent and summed in bfloat16 or wider, within the bound.
No kernel may reach another device: no remote copies, remote signals or barrier semaphores. Data moves between devices by JAX's collectives and lax.ppermute only.
A program may use at most 64 MiB of HBM per device.

v0:
```python
import jax
import jax.numpy as jnp
from jax import lax
from jax.sharding import PartitionSpec as P

KWIN = 256
NTAB = 4
RANGE = 3


def shifted(x, axis, by):
    peers = lax.axis_size(axis)
    pairs = [(i, i + by) for i in range(peers) if 0 <= i + by < peers]
    return lax.ppermute(x, axis, pairs)


def cut_windows(trace_rows, starts):

    def single(trace_row, first_index):
        return lax.dynamic_slice_in_dim(trace_row, first_index, KWIN, 1)

    return jax.vmap(single)(trace_rows, starts)


def bin_windows(windows, slot_ids, active):
    onehot = (slot_ids[:, None] == jnp.arange(NTAB, dtype=jnp.int32)[None, :]) & active[:, None]
    onehot = onehot.astype(jnp.bfloat16)
    return jnp.einsum("it,ifk->tfk", onehot, windows, preferred_element_type=jnp.float32)


def body(traces, tables, slab_range, table_slot, sample_start):
    position = lax.axis_index("slab")
    samples = traces.astype(jnp.bfloat16)
    own_active = (slab_range[:, 0] <= position) & (position <= slab_range[:, 1])
    stacked = bin_windows(
        cut_windows(samples, sample_start[:, RANGE]), table_slot[:, RANGE], own_active
    )
    for offset in list(range(-RANGE, 0)) + list(range(1, RANGE + 1)):
        target = position + offset
        active = (slab_range[:, 0] <= target) & (target <= slab_range[:, 1])
        windows = cut_windows(samples, sample_start[:, offset + RANGE])
        windows = windows * active[:, None, None].astype(jnp.bfloat16)
        arrived_windows, arrived_slots = shifted(
            (windows, table_slot[:, offset + RANGE]), "slab", offset
        )
        everything = jnp.ones(arrived_slots.shape, jnp.bool_)
        stacked = stacked + bin_windows(arrived_windows, arrived_slots, everything)
    binned = stacked.astype(jnp.bfloat16)
    partial_image = jnp.einsum(
        "tfk,tkv->fv",
        binned,
        lax.all_gather(tables, "det", axis=2, tiled=True),
        preferred_element_type=jnp.float32,
    )
    return lax.psum_scatter(partial_image, "det", scatter_dimension=1, tiled=True)


def solution(mesh):
    placed = (
        P(("slab", "det"), None, None),
        P("slab", None, "det"),
        P(("slab", "det"), None),
        P(("slab", "det"), None),
        P(("slab", "det"), None),
    )
    return jax.shard_map(
        body, mesh=mesh, in_specs=placed, out_specs=P(None, ("slab", "det")), check_vma=False
    )
```

profile of v0, /device:TPU:0, one launch (start us, length us, event | category | flops | bytes accessed | tf_op | source)
XLA Modules:
  0.0 129.3 jit_solution(1520195266104620349)
XLA Ops:
  6.5 0.0 all-gather.2.cloned.1.call-start
  6.5 0.7 all-gather.2.cloned.1.call-update
  7.3 0.0 reduce-scatter.2.cloned.1.call-start
  7.3 1.6 %fusion.21 = (s32[1,1]{1,0:T(1,128)}, s32[1,1]{1,0:T(1,128)}, s32[1,1]{1,0:T(1,128)}, s32[1,1]{1,0:T(1,128)}, s32[1,1]{1,0:T(1,128)}, /*index=5*/s32[1,1]{1,0:T(1,128)}, s32[1,1]{1,0:T(1,128)}) fusion(s32[1,7]{1,0:T(1,128)} %param.8), kind=kLoop, calls=%fused_computation.43 | loop fusion | bytes 56 | tf_op jit(solution)/shard_map/slice | solution.py:36
  8.9 3.0 %collective-permute-start.6 = (s32[1]{0:T(128)}, s32[1]{0:T(128)}, u32[]{:S(2)}, u32[]{:S(2)}) collective-permute-start(s32[1]{0:T(128)} %bitcast.33), channel_id=1, source_target_pairs={{0,4},{4,8},{8,12},{12,16},{16,20},{20,24},{24,28},{1,5},{5,9},{9,... | collective-permute-start | bytes 20 | tf_op jit(solution)/shard_map/ppermute | solution.py:14
  11.9 1.3 collective-permute-start.4
  13.1 1.3 collective-permute-start.2
  14.4 1.3 collective-permute-start
  15.7 7.7 %collective-permute-start.10 = (s32[1]{0:T(128)}, s32[1]{0:T(128)}, u32[]{:S(2)}, u32[]{:S(2)}) collective-permute-start(s32[1]{0:T(128)} %bitcast.49), channel_id=1, source_target_pairs={{0,12},{4,16},{8,20},{12,24},{16,28},{1,13},{5,17},{9,21},{13,25},... | collective-permute-start | bytes 20 | tf_op jit(solution)/shard_map/ppermute | solution.py:14
  23.4 1.3 %fusion.23 = (s32[1,1]{1,0:T(1,128)}, s32[1,1]{1,0:T(1,128)}) fusion(s32[1,2]{1,0:T(1,128)} %param.7), kind=kLoop, calls=%fused_computation.45 | loop fusion | bytes 16 | tf_op jit(solution)/shard_map/slice | solution.py:34
  33.7 1.6 %fusion.22 = (s32[1,1]{1,0:T(1,128)}, s32[1,1]{1,0:T(1,128)}, s32[1,1]{1,0:T(1,128)}, s32[1,1]{1,0:T(1,128)}, s32[1,1]{1,0:T(1,128)}, /*index=5*/s32[1,1]{1,0:T(1,128)}, s32[1,1]{1,0:T(1,128)}) fusion(s32[1,7]{1,0:T(1,128)} %param.9), kind=kLoop, calls=%fused_computation.44 | loop fusion | bytes 56 | tf_op jit(solution)/shard_map/slice | solution.py:36
  44.2 1.7 %convert_element_type.10 = bf16[1,128,4096]{2,1,0:T(8,128)(2,1)S(1)} convert(f32[1,128,4096]{2,1,0:T(8,128)} %param.5) | non-fusion elementwise | flops 524288 | bytes 3145728 | tf_op jit(solution)/shard_map/convert_element_type | solution.py:33
  50.4 0.6 fusion.14
  51.0 0.2 bitcast_convert_fusion.6
  51.2 0.0 collective-permute-done.6
  51.2 5.9 %collective-permute-start.8 = (s32[1]{0:T(128)}, s32[1]{0:T(128)}, u32[]{:S(2)}, u32[]{:S(2)}) collective-permute-start(s32[1]{0:T(128)} %bitcast.41), channel_id=1, source_target_pairs={{0,8},{4,12},{8,16},{12,20},{16,24},{20,28},{1,9},{5,13},{9,17},{1... | collective-permute-start | bytes 20 | tf_op jit(solution)/shard_map/ppermute | solution.py:14
  57.1 0.7 fusion.18
  57.8 0.0 collective-permute-done.4
  57.8 1.3 %collective-permute-start.11 = (bf16[1,128,256]{2,1,0:T(8,128)(2,1)S(1)}, bf16[1,128,256]{2,1,0:T(8,128)(2,1)S(1)}, u32[]{:S(2)}, u32[]{:S(2)}) collective-permute-start(bf16[1,128,256]{2,1,0:T(8,128)(2,1)S(1)} %get-tuple-element.83), channel_id=1, source_target_pairs={{0,12},{4,16},{8,20},{12,24},{16,28},{1,13},{5,17},{9,21},{13,25},... | collective-permute-start | bytes 196616 | tf_op jit(solution)/shard_map/ppermute | solution.py:14
  59.1 0.6 fusion.17
  59.8 0.0 collective-permute-done.2
  59.8 2.9 %collective-permute-start.9 = (bf16[1,128,256]{2,1,0:T(8,128)(2,1)S(1)}, bf16[1,128,256]{2,1,0:T(8,128)(2,1)S(1)}, u32[]{:S(2)}, u32[]{:S(2)}) collective-permute-start(bf16[1,128,256]{2,1,0:T(8,128)(2,1)S(1)} %get-tuple-element.84), channel_id=1, source_target_pairs={{0,8},{4,12},{8,16},{12,20},{16,24},{20,28},{1,9},{5,13},{9,17},{1... | collective-permute-start | bytes 196616 | tf_op jit(solution)/shard_map/ppermute | solution.py:14
  62.6 0.6 fusion.16
  63.3 0.0 collective-permute-done
  63.3 1.3 %collective-permute-start.7 = (bf16[1,128,256]{2,1,0:T(8,128)(2,1)S(1)}, bf16[1,128,256]{2,1,0:T(8,128)(2,1)S(1)}, u32[]{:S(2)}, u32[]{:S(2)}) collective-permute-start(bf16[1,128,256]{2,1,0:T(8,128)(2,1)S(1)} %get-tuple-element.85), channel_id=1, source_target_pairs={{0,4},{4,8},{8,12},{12,16},{16,20},{20,24},{24,28},{1,5},{5,9},{9,... | collective-permute-start | bytes 196616 | tf_op jit(solution)/shard_map/ppermute | solution.py:14
  64.6 0.6 fusion.15
  65.2 0.0 collective-permute-done.10
  65.3 1.3 collective-permute-start.5
  66.6 0.6 fusion.20
  67.2 0.0 collective-permute-done.8
  67.2 1.3 collective-permute-start.3
  68.5 0.7 fusion.19
  69.2 0.0 collective-permute-done.11
  69.2 1.3 collective-permute-start.1
  70.5 0.0 collective-permute-done.9
  70.5 0.0 collective-permute-done.7
  70.6 0.0 collective-permute-done.5
  70.6 4.5 %collective-permute-done.3 = bf16[1,128,256]{2,1,0:T(8,128)(2,1)S(1)} collective-permute-done((bf16[1,128,256]{2,1,0:T(8,128)(2,1)S(1)}, bf16[1,128,256]{2,1,0:T(8,128)(2,1)S(1)}, u32[]{:S(2)}, u32[]{:S(2)}) %collective-permute-start.3) | collective-permute-done | bytes 65568 | tf_op jit(solution)/shard_map/ppermute | solution.py:14
  75.1 1.9 %collective-permute-done.1 = bf16[1,128,256]{2,1,0:T(8,128)(2,1)S(1)} collective-permute-done((bf16[1,128,256]{2,1,0:T(8,128)(2,1)S(1)}, bf16[1,128,256]{2,1,0:T(8,128)(2,1)S(1)}, u32[]{:S(2)}, u32[]{:S(2)}) %collective-permute-start.1) | collective-permute-done | bytes 65568 | tf_op jit(solution)/shard_map/ppermute | solution.py:14
  77.0 15.4 %all-gather.2.cloned.1.call-done = bf16[4,256,2048]{2,1,0:T(8,128)(2,1)} async-done(((bf16[4,256,512]{2,1,0:T(8,128)(2,1)}), bf16[4,256,2048]{2,1,0:T(8,128)(2,1)}) %all-gather.2.cloned.1.call-update) | async-done | bytes 4194320 | tf_op jit(solution)/shard_map/all_gather | solution.py:52
  92.4 4.1 %convolution_bitcast_fusion = f32[128,2048]{1,0:T(8,128)} fusion(bf16[4,256,2048]{2,1,0:T(8,128)(2,1)} %all-gather.2.cloned.1.call-done, f32[128,256]{1,0:T(8,128)S(1)} %bitcast_convert_fusion, f32[4]{0:T(128)S(1)} %fusion.20, f32[128,256]{1,0:T(8,128)S(1)} %bitcast_convert_fusion.1, f32[4]{0:T(128)S(1)} %fusion.19, f32[128,256]{1,0:T(8,128)S(1)} %bitcast_convert_fusion.2, ...), kind=kOutput, calls=%fused_computation | convolution fusion | flops 538705920 | bytes 6160496 | tf_op jit(solution)/shard_map/tfk,tkv->fv/dot_general | solution.py:49
  96.5 0.0 reduce-scatter.2.cloned.1.call-update
  96.5 25.9 %reduce-scatter.2.cloned.1.call-done = f32[128,512]{1,0:T(8,128)} async-done(((f32[128,2048]{1,0:T(8,128)}), f32[128,512]{1,0:T(8,128)}) %reduce-scatter.2.cloned.1.call-update) | async-done | bytes 262160 | tf_op jit(solution)/shard_map/reduce_scatter | solution.py:55
  (6 shorter events, 0.1 us)
Async XLA Ops:
  6.5 85.9 %all-gather.2.cloned.1.call-start = ((), (), s32[]{:S(2)}) async-start(), calls=%async_computation.1 | async-start | bytes 5242880 | tf_op jit(solution)/shard_map/all_gather | solution.py:52
  7.3 115.2 %reduce-scatter.2.cloned.1.call-start = ((), (), s32[]{:S(2)}) async-start(), calls=%async_computation.2 | async-start | bytes 1310720 | tf_op jit(solution)/shard_map/reduce_scatter | solution.py:55
  8.9 42.3 %collective-permute-start.6 = (s32[1]{0:T(128)}, s32[1]{0:T(128)}, u32[]{:S(2)}, u32[]{:S(2)}) collective-permute-start(s32[1]{0:T(128)} %bitcast.33), channel_id=1, source_target_pairs={{0,4},{4,8},{8,12},{12,16},{16,20},{20,24},{24,28},{1,5},{5,9},{9,... | collective-permute-start | bytes 20 | tf_op jit(solution)/shard_map/ppermute | solution.py:14
  11.9 46.0 %collective-permute-start.4 = (s32[1]{0:T(128)}, s32[1]{0:T(128)}, u32[]{:S(2)}, u32[]{:S(2)}) collective-permute-start(s32[1]{0:T(128)} %bitcast.25), channel_id=1, source_target_pairs={{4,0},{8,4},{12,8},{16,12},{20,16},{24,20},{28,24},{5,1},{9,5},{13... | collective-permute-start | bytes 20 | tf_op jit(solution)/shard_map/ppermute | solution.py:14
  13.1 46.6 %collective-permute-start.2 = (s32[1]{0:T(128)}, s32[1]{0:T(128)}, u32[]{:S(2)}, u32[]{:S(2)}) collective-permute-start(s32[1]{0:T(128)} %bitcast.17), channel_id=1, source_target_pairs={{8,0},{12,4},{16,8},{20,12},{24,16},{28,20},{9,1},{13,5},{17,9},{2... | collective-permute-start | bytes 20 | tf_op jit(solution)/shard_map/ppermute | solution.py:14
  14.4 48.8 %collective-permute-start = (s32[1]{0:T(128)}, s32[1]{0:T(128)}, u32[]{:S(2)}, u32[]{:S(2)}) collective-permute-start(s32[1]{0:T(128)} %bitcast.9), channel_id=1, source_target_pairs={{12,0},{16,4},{20,8},{24,12},{28,16},{13,1},{17,5},{21,9},{25,13},... | collective-permute-start | bytes 20 | tf_op jit(solution)/shard_map/ppermute | solution.py:14
  15.7 49.5 %collective-permute-start.10 = (s32[1]{0:T(128)}, s32[1]{0:T(128)}, u32[]{:S(2)}, u32[]{:S(2)}) collective-permute-start(s32[1]{0:T(128)} %bitcast.49), channel_id=1, source_target_pairs={{0,12},{4,16},{8,20},{12,24},{16,28},{1,13},{5,17},{9,21},{13,25},... | collective-permute-start | bytes 20 | tf_op jit(solution)/shard_map/ppermute | solution.py:14
  51.2 16.0 %collective-permute-start.8 = (s32[1]{0:T(128)}, s32[1]{0:T(128)}, u32[]{:S(2)}, u32[]{:S(2)}) collective-permute-start(s32[1]{0:T(128)} %bitcast.41), channel_id=1, source_target_pairs={{0,8},{4,12},{8,16},{12,20},{16,24},{20,28},{1,9},{5,13},{9,17},{1... | collective-permute-start | bytes 20 | tf_op jit(solution)/shard_map/ppermute | solution.py:14
  57.8 11.4 %collective-permute-start.11 = (bf16[1,128,256]{2,1,0:T(8,128)(2,1)S(1)}, bf16[1,128,256]{2,1,0:T(8,128)(2,1)S(1)}, u32[]{:S(2)}, u32[]{:S(2)}) collective-permute-start(bf16[1,128,256]{2,1,0:T(8,128)(2,1)S(1)} %get-tuple-element.83), channel_id=1, source_target_pairs={{0,12},{4,16},{8,20},{12,24},{16,28},{1,13},{5,17},{9,21},{13,25},... | collective-permute-start | bytes 196616 | tf_op jit(solution)/shard_map/ppermute | solution.py:14
  59.8 10.7 %collective-permute-start.9 = (bf16[1,128,256]{2,1,0:T(8,128)(2,1)S(1)}, bf16[1,128,256]{2,1,0:T(8,128)(2,1)S(1)}, u32[]{:S(2)}, u32[]{:S(2)}) collective-permute-start(bf16[1,128,256]{2,1,0:T(8,128)(2,1)S(1)} %get-tuple-element.84), channel_id=1, source_target_pairs={{0,8},{4,12},{8,16},{12,20},{16,24},{20,28},{1,9},{5,13},{9,17},{1... | collective-permute-start | bytes 196616 | tf_op jit(solution)/shard_map/ppermute | solution.py:14
  63.3 7.2 %collective-permute-start.7 = (bf16[1,128,256]{2,1,0:T(8,128)(2,1)S(1)}, bf16[1,128,256]{2,1,0:T(8,128)(2,1)S(1)}, u32[]{:S(2)}, u32[]{:S(2)}) collective-permute-start(bf16[1,128,256]{2,1,0:T(8,128)(2,1)S(1)} %get-tuple-element.85), channel_id=1, source_target_pairs={{0,4},{4,8},{8,12},{12,16},{16,20},{20,24},{24,28},{1,5},{5,9},{9,... | collective-permute-start | bytes 196616 | tf_op jit(solution)/shard_map/ppermute | solution.py:14
  65.3 5.3 %collective-permute-start.5 = (bf16[1,128,256]{2,1,0:T(8,128)(2,1)S(1)}, bf16[1,128,256]{2,1,0:T(8,128)(2,1)S(1)}, u32[]{:S(2)}, u32[]{:S(2)}) collective-permute-start(bf16[1,128,256]{2,1,0:T(8,128)(2,1)S(1)} %get-tuple-element.86), channel_id=1, source_target_pairs={{4,0},{8,4},{12,8},{16,12},{20,16},{24,20},{28,24},{5,1},{9,5},{13... | collective-permute-start | bytes 196616 | tf_op jit(solution)/shard_map/ppermute | solution.py:14
  67.2 7.9 %collective-permute-start.3 = (bf16[1,128,256]{2,1,0:T(8,128)(2,1)S(1)}, bf16[1,128,256]{2,1,0:T(8,128)(2,1)S(1)}, u32[]{:S(2)}, u32[]{:S(2)}) collective-permute-start(bf16[1,128,256]{2,1,0:T(8,128)(2,1)S(1)} %get-tuple-element.87), channel_id=1, source_target_pairs={{8,0},{12,4},{16,8},{20,12},{24,16},{28,20},{9,1},{13,5},{17,9},{2... | collective-permute-start | bytes 196616 | tf_op jit(solution)/shard_map/ppermute | solution.py:14
  69.2 7.8 %collective-permute-start.1 = (bf16[1,128,256]{2,1,0:T(8,128)(2,1)S(1)}, bf16[1,128,256]{2,1,0:T(8,128)(2,1)S(1)}, u32[]{:S(2)}, u32[]{:S(2)}) collective-permute-start(bf16[1,128,256]{2,1,0:T(8,128)(2,1)S(1)} %get-tuple-element.88), channel_id=1, source_target_pairs={{12,0},{16,4},{20,8},{24,12},{28,16},{13,1},{17,5},{21,9},{25,13},... | collective-permute-start | bytes 196616 | tf_op jit(solution)/shard_map/ppermute | solution.py:14
Sparse Core Ops, SparseCore 0:
  8.9 83.4 all-gather.1
  96.6 25.7 reduce-scatter.1
where the time goes:
time: 130 us; the launch traced here: 129 us
  waiting for transfers between devices  48.5 us (37%)
  between operations  36 us (28%)
  starting transfers between devices  29.8 us (23%)
  other arithmetic  6.48 us (5%)
  local copies, waits for them, and re-layouts  4.5 us (3%)
  matrix products  4.07 us (3%)
    ppermute x12, starting transfers between devices, shifted(): return lax.ppermute(x, axis, pairs)  29.8 us
    reduce_scatter x1, waiting for transfers between devices, body(): lax.psum_scatter(partial_image, 'det', scatter_dimension=1, tiled=True)  25.9 us
    all_gather x1, waiting for transfers between devices, body(): lax.all_gather(tables, 'det', axis=2, tiled=True)  15.4 us
    ppermute x12, waiting for transfers between devices, shifted(): return lax.ppermute(x, axis, pairs)  6.42 us
    another operation x14, other arithmetic  4.75 us
    dot_general x1, matrix products, body(): jnp.einsum('tfk,tkv->fv', binned, lax.all_gather(tables, 'det', axis=2, t...  4.07 us
  transfers between devices with their start and end apart: 14, of which 4 were waited for; matrix products, arithmetic and copies ran while one was open for 8% of the time, Pallas kernels for 0%

commit v1 on v0

--- a/solution.py
+++ b/solution.py
@@ -49,7 +49,9 @@
     partial_image = jnp.einsum(
         "tfk,tkv->fv",
         binned,
-        lax.all_gather(tables, "det", axis=2, tiled=True),
+        jnp.concatenate(
+            lax.all_to_all(jnp.stack([tables] * lax.axis_size("det")), "det", 0, 0), axis=2
+        ),
         preferred_element_type=jnp.float32,
     )
     return lax.psum_scatter(partial_image, "det", scatter_dimension=1, tiled=True)

time: 130 us -> 149 us (1.15)
  waiting for transfers between devices: 48.5 us -> 67.3 us
  local copies, waits for them, and re-layouts: 4.5 us -> 8.47 us
  matrix products: 4.07 us -> 1.99 us
  other arithmetic: 6.48 us -> 4.87 us
    all_to_all x0 -> x1, waiting for transfers between devices: none -> 25.7 us  [body(): lax.all_to_all(jnp.stack([tables] * lax.axis_size('det')), 'det', 0, 0)]
    all_gather x1 -> x0, waiting for transfers between devices: 15.4 us -> none  [body(): lax.all_gather(tables, 'det', axis=2, tiled=True)]
    ppermute x12, waiting for transfers between devices: 6.42 us -> 15 us  [shifted(): return lax.ppermute(x, axis, pairs)]
    all_to_all x0 -> x1, starting transfers between devices: none -> 6.48 us  [body(): lax.all_to_all(jnp.stack([tables] * lax.axis_size('det')), 'det', 0, 0)]
    ppermute x12, starting transfers between devices: 29.8 us -> 23.8 us  [shifted(): return lax.ppermute(x, axis, pairs)]
    another operation x0 -> x1, local copies, waits for them, and re-layouts: none -> 3.65 us  [body(): jnp.stack([tables] * lax.axis_size('det'))]
    reshape x0 -> x1, local copies, waits for them, and re-layouts: none -> 2.82 us  [body(): jnp.concatenate(lax.all_to_all(jnp.stack([tables] * lax.axis_size('det'))...]
    dot_general x1, matrix products: 4.07 us -> 1.99 us  [body(): jnp.einsum('tfk,tkv->fv', binned, jnp.concatenate(lax.all_to_all(jnp.stac...]
  transfers between devices with their start and end apart: 14 -> 14, of which waited for: 4 -> 7; matrix products, arithmetic and copies ran while one was open for 8% -> 5% of each run, Pallas kernels for 0% -> 0%
where the time goes in v1:
time: 149 us; the launch traced here: 148 us
  waiting for transfers between devices  67.3 us (45%)
  between operations  35.5 us (24%)
  starting transfers between devices  30.2 us (20%)
  local copies, waits for them, and re-layouts  8.47 us (6%)
  other arithmetic  4.87 us (3%)
  matrix products  1.99 us (1%)
    reduce_scatter x1, waiting for transfers between devices, body(): lax.psum_scatter(partial_image, 'det', scatter_dimension=1, tiled=True)  26.6 us
    all_to_all x1, waiting for transfers between devices, body(): lax.all_to_all(jnp.stack([tables] * lax.axis_size('det')), 'det', 0, 0)  25.7 us
    ppermute x12, starting transfers between devices, shifted(): return lax.ppermute(x, axis, pairs)  23.8 us
    ppermute x12, waiting for transfers between devices, shifted(): return lax.ppermute(x, axis, pairs)  15 us
    all_to_all x1, starting transfers between devices, body(): lax.all_to_all(jnp.stack([tables] * lax.axis_size('det')), 'det', 0, 0)  6.48 us
    another operation x14, other arithmetic  4.75 us
    another operation x1, local copies, waits for them, and re-layouts, body(): jnp.stack([tables] * lax.axis_size('det'))  3.65 us
  transfers between devices with their start and end apart: 14, of which 7 were waited for; matrix products, arithmetic and copies ran while one was open for 5% of the time, Pallas kernels for 0%

profile of v1, /device:TPU:0, one launch (start us, length us, event | category | flops | bytes accessed | tf_op | source)
XLA Modules:
  0.0 148.4 jit_solution(17847689670811492156)
XLA Ops:
  6.5 3.7 %stack.2 = bf16[4,4,256,512]{3,2,1,0:T(8,128)(2,1)} broadcast(bf16[4,256,512]{2,1,0:T(8,128)(2,1)} %param.6), dimensions={1,2,3} | broadcast | bytes 5242880 | tf_op jit(solution)/shard_map/stack | solution.py:53
  10.2 6.5 %all-to-all-start = ((bf16[4,4,256,512]{3,2,1,0:T(8,128)(2,1)}), bf16[4,4,256,512]{3,2,1,0:T(8,128)(2,1)}, u32[]{:S(2)}, u32[]{:S(2)}) async-start(bf16[4,4,256,512]{3,2,1,0:T(8,128)(2,1)} %stack.2), calls=%async_computation | async-start | bytes 8388608 | tf_op jit(solution)/shard_map/all_to_all | solution.py:53
  16.7 0.0 reduce-scatter.2.cloned.1.call-start
  16.7 0.0 copy-done.1
  16.7 0.7 fusion.22
  19.8 0.0 copy-done.3
  19.8 0.6 fusion.23
  34.1 0.0 copy-done
  34.1 0.1 convert_element_type.10
  38.8 0.2 bitcast_convert_fusion.6
  39.0 2.9 %collective-permute-start.11 = (bf16[1,128,256]{2,1,0:T(8,128)(2,1)S(1)}, bf16[1,128,256]{2,1,0:T(8,128)(2,1)S(1)}, u32[]{:S(2)}, u32[]{:S(2)}) collective-permute-start(bf16[1,128,256]{2,1,0:T(8,128)(2,1)S(1)} %get-tuple-element.83), channel_id=1, source_target_pairs={{0,12},{4,16},{8,20},{12,24},{16,28},{1,13},{5,17},{9,21},{13,25},... | collective-permute-start | bytes 196616 | tf_op jit(solution)/shard_map/ppermute | solution.py:14
  41.9 0.0 copy-done.2
  42.0 0.7 fusion.21
  42.6 4.3 %collective-permute-start.10 = (s32[1]{0:T(128)}, s32[1]{0:T(128)}, u32[]{:S(2)}, u32[]{:S(2)}) collective-permute-start(s32[1]{0:T(128)} %bitcast.49), channel_id=1, source_target_pairs={{0,12},{4,16},{8,20},{12,24},{16,28},{1,13},{5,17},{9,21},{13,25},... | collective-permute-start | bytes 20 | tf_op jit(solution)/shard_map/ppermute | solution.py:14
  46.9 1.3 collective-permute-start.9
  48.2 3.7 %collective-permute-start.8 = (s32[1]{0:T(128)}, s32[1]{0:T(128)}, u32[]{:S(2)}, u32[]{:S(2)}) collective-permute-start(s32[1]{0:T(128)} %bitcast.41), channel_id=1, source_target_pairs={{0,8},{4,12},{8,16},{12,20},{16,24},{20,28},{1,9},{5,13},{9,17},{1... | collective-permute-start | bytes 20 | tf_op jit(solution)/shard_map/ppermute | solution.py:14
  51.9 1.3 collective-permute-start.7
  54.4 0.7 fusion.14
  55.0 0.0 collective-permute-done.10
  55.1 2.6 %collective-permute-start.6 = (s32[1]{0:T(128)}, s32[1]{0:T(128)}, u32[]{:S(2)}, u32[]{:S(2)}) collective-permute-start(s32[1]{0:T(128)} %bitcast.33), channel_id=1, source_target_pairs={{0,4},{4,8},{8,12},{12,16},{16,20},{20,24},{24,28},{1,5},{5,9},{9,... | collective-permute-start | bytes 20 | tf_op jit(solution)/shard_map/ppermute | solution.py:14
  57.7 0.6 fusion.20
  58.3 0.0 collective-permute-done.8
  58.3 1.3 collective-permute-start.5
  59.6 0.6 fusion.19
  60.3 0.0 collective-permute-done.6
  60.3 1.3 collective-permute-start.4
  61.6 0.6 fusion.18
  62.1 2.0 %collective-permute-done.4 = s32[1]{0:T(128)} collective-permute-done((s32[1]{0:T(128)}, s32[1]{0:T(128)}, u32[]{:S(2)}, u32[]{:S(2)}) %collective-permute-start.4) | collective-permute-done | bytes 36 | tf_op jit(solution)/shard_map/ppermute | solution.py:14
  64.1 1.3 collective-permute-start.2
  65.4 0.6 fusion.17
  66.1 3.6 %collective-permute-done.2 = s32[1]{0:T(128)} collective-permute-done((s32[1]{0:T(128)}, s32[1]{0:T(128)}, u32[]{:S(2)}, u32[]{:S(2)}) %collective-permute-start.2) | collective-permute-done | bytes 36 | tf_op jit(solution)/shard_map/ppermute | solution.py:14
  69.7 1.3 collective-permute-start
  71.0 0.6 fusion.16
  71.7 3.8 %collective-permute-done = s32[1]{0:T(128)} collective-permute-done((s32[1]{0:T(128)}, s32[1]{0:T(128)}, u32[]{:S(2)}, u32[]{:S(2)}) %collective-permute-start) | collective-permute-done | bytes 36 | tf_op jit(solution)/shard_map/ppermute | solution.py:14
  75.5 1.3 collective-permute-start.3
  76.8 0.7 fusion.15
  77.5 0.0 collective-permute-done.11
  77.5 1.3 collective-permute-start.1
  78.8 0.0 collective-permute-done.9
  78.8 0.0 collective-permute-done.7
  78.8 0.0 collective-permute-done.5
  78.9 3.8 %collective-permute-done.3 = bf16[1,128,256]{2,1,0:T(8,128)(2,1)S(1)} collective-permute-done((bf16[1,128,256]{2,1,0:T(8,128)(2,1)S(1)}, bf16[1,128,256]{2,1,0:T(8,128)(2,1)S(1)}, u32[]{:S(2)}, u32[]{:S(2)}) %collective-permute-start.3) | collective-permute-done | bytes 65568 | tf_op jit(solution)/shard_map/ppermute | solution.py:14
  82.7 1.6 %collective-permute-done.1 = bf16[1,128,256]{2,1,0:T(8,128)(2,1)S(1)} collective-permute-done((bf16[1,128,256]{2,1,0:T(8,128)(2,1)S(1)}, bf16[1,128,256]{2,1,0:T(8,128)(2,1)S(1)}, u32[]{:S(2)}, u32[]{:S(2)}) %collective-permute-start.1) | collective-permute-done | bytes 65568 | tf_op jit(solution)/shard_map/ppermute | solution.py:14
  84.4 25.7 %all-to-all-done = bf16[4,4,256,512]{3,2,1,0:T(8,128)(2,1)} async-done(((bf16[4,4,256,512]{3,2,1,0:T(8,128)(2,1)}), bf16[4,4,256,512]{3,2,1,0:T(8,128)(2,1)}, u32[]{:S(2)}, u32[]{:S(2)}) %all-to-all-start) | async-done | bytes 4194336 | tf_op jit(solution)/shard_map/all_to_all | solution.py:53
  110.1 2.8 %copy.7 = bf16[4,4,32,8,512]{4,3,0,2,1:T(8,128)(2,1)S(1)} copy(bf16[4,4,32,8,512]{4,3,2,1,0:T(8,128)(2,1)} %bitcast.66) | data formatting | bytes 8388608 | tf_op jit(solution)/shard_map/reshape | solution.py:52
  112.9 2.0 %convolution_bitcast_fusion = f32[128,2048]{1,0:T(8,128)} fusion(bf16[4,256,2048]{2,1,0:T(8,128)(2,1)S(1)} %bitcast.84, f32[128,256]{1,0:T(8,128)S(1)} %bitcast_convert_fusion, f32[4]{0:T(128)S(1)} %fusion.20, f32[128,256]{1,0:T(8,128)S(1)} %bitcast_convert_fusion.1, f32[4]{0:T(128)S(1)} %fusion.19, f32[128,256]{1,0:T(8,128)S(1)} %bitcast_convert_fusion.2, ...), kind=kOutput, calls=%fused_computation | convolution fusion | flops 538705920 | bytes 6160496 | tf_op jit(solution)/shard_map/tfk,tkv->fv/dot_general | solution.py:49
  114.9 0.0 reduce-scatter.2.cloned.1.call-update
  114.9 26.6 %reduce-scatter.2.cloned.1.call-done = f32[128,512]{1,0:T(8,128)} async-done(((f32[128,2048]{1,0:T(8,128)}), f32[128,512]{1,0:T(8,128)}) %reduce-scatter.2.cloned.1.call-update) | async-done | bytes 262160 | tf_op jit(solution)/shard_map/reduce_scatter | solution.py:57
  (10 shorter events, 0.1 us)
Async XLA Ops:
  10.2 6.5 %copy-start.1 = (s32[1,7]{1,0:T(1,128)S(1)}, s32[1,7]{1,0:T(1,128)}, u32[]{:S(2)}) copy-start(s32[1,7]{1,0:T(1,128)} %param.9) | copy-start | bytes 88
  10.2 9.6 %copy-start.3 = (s32[1,2]{1,0:T(1,128)S(1)}, s32[1,2]{1,0:T(1,128)}, u32[]{:S(2)}) copy-start(s32[1,2]{1,0:T(1,128)} %param.7) | copy-start | bytes 28
  10.2 23.9 %copy-start = (f32[1,128,4096]{2,1,0:T(8,128)S(1)}, f32[1,128,4096]{2,1,0:T(8,128)}, u32[]{:S(2)}) copy-start(f32[1,128,4096]{2,1,0:T(8,128)} %param.5) | copy-start | bytes 6291460
  10.2 99.9 %all-to-all-start = ((bf16[4,4,256,512]{3,2,1,0:T(8,128)(2,1)}), bf16[4,4,256,512]{3,2,1,0:T(8,128)(2,1)}, u32[]{:S(2)}, u32[]{:S(2)}) async-start(bf16[4,4,256,512]{3,2,1,0:T(8,128)(2,1)} %stack.2), calls=%async_computation | async-start | bytes 8388608 | tf_op jit(solution)/shard_map/all_to_all | solution.py:53
  16.7 25.3 %copy-start.2 = (s32[1,7]{1,0:T(1,128)S(1)}, s32[1,7]{1,0:T(1,128)}, u32[]{:S(2)}) copy-start(s32[1,7]{1,0:T(1,128)} %param.8) | copy-start | bytes 88
  16.7 124.9 %reduce-scatter.2.cloned.1.call-start = ((), (), s32[]{:S(2)}) async-start(), calls=%async_computation.2 | async-start | bytes 1310720 | tf_op jit(solution)/shard_map/reduce_scatter | solution.py:57
  39.0 38.4 %collective-permute-start.11 = (bf16[1,128,256]{2,1,0:T(8,128)(2,1)S(1)}, bf16[1,128,256]{2,1,0:T(8,128)(2,1)S(1)}, u32[]{:S(2)}, u32[]{:S(2)}) collective-permute-start(bf16[1,128,256]{2,1,0:T(8,128)(2,1)S(1)} %get-tuple-element.83), channel_id=1, source_target_pairs={{0,12},{4,16},{8,20},{12,24},{16,28},{1,13},{5,17},{9,21},{13,25},... | collective-permute-start | bytes 196616 | tf_op jit(solution)/shard_map/ppermute | solution.py:14
  42.6 12.4 %collective-permute-start.10 = (s32[1]{0:T(128)}, s32[1]{0:T(128)}, u32[]{:S(2)}, u32[]{:S(2)}) collective-permute-start(s32[1]{0:T(128)} %bitcast.49), channel_id=1, source_target_pairs={{0,12},{4,16},{8,20},{12,24},{16,28},{1,13},{5,17},{9,21},{13,25},... | collective-permute-start | bytes 20 | tf_op jit(solution)/shard_map/ppermute | solution.py:14
  46.9 31.9 %collective-permute-start.9 = (bf16[1,128,256]{2,1,0:T(8,128)(2,1)S(1)}, bf16[1,128,256]{2,1,0:T(8,128)(2,1)S(1)}, u32[]{:S(2)}, u32[]{:S(2)}) collective-permute-start(bf16[1,128,256]{2,1,0:T(8,128)(2,1)S(1)} %get-tuple-element.84), channel_id=1, source_target_pairs={{0,8},{4,12},{8,16},{12,20},{16,24},{20,28},{1,9},{5,13},{9,17},{1... | collective-permute-start | bytes 196616 | tf_op jit(solution)/shard_map/ppermute | solution.py:14
  48.2 10.1 %collective-permute-start.8 = (s32[1]{0:T(128)}, s32[1]{0:T(128)}, u32[]{:S(2)}, u32[]{:S(2)}) collective-permute-start(s32[1]{0:T(128)} %bitcast.41), channel_id=1, source_target_pairs={{0,8},{4,12},{8,16},{12,20},{16,24},{20,28},{1,9},{5,13},{9,17},{1... | collective-permute-start | bytes 20 | tf_op jit(solution)/shard_map/ppermute | solution.py:14
  51.9 26.9 %collective-permute-start.7 = (bf16[1,128,256]{2,1,0:T(8,128)(2,1)S(1)}, bf16[1,128,256]{2,1,0:T(8,128)(2,1)S(1)}, u32[]{:S(2)}, u32[]{:S(2)}) collective-permute-start(bf16[1,128,256]{2,1,0:T(8,128)(2,1)S(1)} %get-tuple-element.85), channel_id=1, source_target_pairs={{0,4},{4,8},{8,12},{12,16},{16,20},{20,24},{24,28},{1,5},{5,9},{9,... | collective-permute-start | bytes 196616 | tf_op jit(solution)/shard_map/ppermute | solution.py:14
  55.1 5.2 %collective-permute-start.6 = (s32[1]{0:T(128)}, s32[1]{0:T(128)}, u32[]{:S(2)}, u32[]{:S(2)}) collective-permute-start(s32[1]{0:T(128)} %bitcast.33), channel_id=1, source_target_pairs={{0,4},{4,8},{8,12},{12,16},{16,20},{20,24},{24,28},{1,5},{5,9},{9,... | collective-permute-start | bytes 20 | tf_op jit(solution)/shard_map/ppermute | solution.py:14
  58.3 20.5 %collective-permute-start.5 = (bf16[1,128,256]{2,1,0:T(8,128)(2,1)S(1)}, bf16[1,128,256]{2,1,0:T(8,128)(2,1)S(1)}, u32[]{:S(2)}, u32[]{:S(2)}) collective-permute-start(bf16[1,128,256]{2,1,0:T(8,128)(2,1)S(1)} %get-tuple-element.86), channel_id=1, source_target_pairs={{4,0},{8,4},{12,8},{16,12},{20,16},{24,20},{28,24},{5,1},{9,5},{13... | collective-permute-start | bytes 196616 | tf_op jit(solution)/shard_map/ppermute | solution.py:14
  60.3 3.9 %collective-permute-start.4 = (s32[1]{0:T(128)}, s32[1]{0:T(128)}, u32[]{:S(2)}, u32[]{:S(2)}) collective-permute-start(s32[1]{0:T(128)} %bitcast.25), channel_id=1, source_target_pairs={{4,0},{8,4},{12,8},{16,12},{20,16},{24,20},{28,24},{5,1},{9,5},{13... | collective-permute-start | bytes 20 | tf_op jit(solution)/shard_map/ppermute | solution.py:14
  64.1 5.6 %collective-permute-start.2 = (s32[1]{0:T(128)}, s32[1]{0:T(128)}, u32[]{:S(2)}, u32[]{:S(2)}) collective-permute-start(s32[1]{0:T(128)} %bitcast.17), channel_id=1, source_target_pairs={{8,0},{12,4},{16,8},{20,12},{24,16},{28,20},{9,1},{13,5},{17,9},{2... | collective-permute-start | bytes 20 | tf_op jit(solution)/shard_map/ppermute | solution.py:14
  69.7 5.7 %collective-permute-start = (s32[1]{0:T(128)}, s32[1]{0:T(128)}, u32[]{:S(2)}, u32[]{:S(2)}) collective-permute-start(s32[1]{0:T(128)} %bitcast.9), channel_id=1, source_target_pairs={{12,0},{16,4},{20,8},{24,12},{28,16},{13,1},{17,5},{21,9},{25,13},... | collective-permute-start | bytes 20 | tf_op jit(solution)/shard_map/ppermute | solution.py:14
  75.5 7.2 %collective-permute-start.3 = (bf16[1,128,256]{2,1,0:T(8,128)(2,1)S(1)}, bf16[1,128,256]{2,1,0:T(8,128)(2,1)S(1)}, u32[]{:S(2)}, u32[]{:S(2)}) collective-permute-start(bf16[1,128,256]{2,1,0:T(8,128)(2,1)S(1)} %get-tuple-element.87), channel_id=1, source_target_pairs={{8,0},{12,4},{16,8},{20,12},{24,16},{28,20},{9,1},{13,5},{17,9},{2... | collective-permute-start | bytes 196616 | tf_op jit(solution)/shard_map/ppermute | solution.py:14
  77.5 6.9 %collective-permute-start.1 = (bf16[1,128,256]{2,1,0:T(8,128)(2,1)S(1)}, bf16[1,128,256]{2,1,0:T(8,128)(2,1)S(1)}, u32[]{:S(2)}, u32[]{:S(2)}) collective-permute-start(bf16[1,128,256]{2,1,0:T(8,128)(2,1)S(1)} %get-tuple-element.88), channel_id=1, source_target_pairs={{12,0},{16,4},{20,8},{24,12},{28,16},{13,1},{17,5},{21,9},{25,13},... | collective-permute-start | bytes 196616 | tf_op jit(solution)/shard_map/ppermute | solution.py:14
Sparse Core Ops, SparseCore 0:
  115.1 26.4 reduce-scatter.1
